TPU v7x, 32 devices: a whole 2x2x4 slice. The times are simulated.
32 devices in a mesh: grp: 2 (over x), seq: 16 (over z, y, core).
Axes of the slice: x: 2, y: 2, z: 4, core: 2. Of those that a mesh axis runs over, the one named last changes fastest.
Arguments:
- queries: bfloat16 [256, 4096], P(('grp', 'seq')), parts along dimension 0, may hold values from -9 to 9
- question_keys: bfloat16 [256, 2048], P(('grp', 'seq')), parts along dimension 0, may hold values from -4 to 4
- question_values: bfloat16 [256, 2048], P(('grp', 'seq')), parts along dimension 0, may hold values from -5 to 5
- doc_keys: bfloat16 [16384, 2048], P(('grp', 'seq')), parts along dimension 0, may hold values from -4 to 4
- doc_values: bfloat16 [16384, 2048], P(('grp', 'seq')), parts along dimension 0, may hold values from -5 to 5
- lengths: int32 [2], P('grp'), parts along dimension 0, may hold values from 4 to 128
- offsets: int32 [2], P('grp'), parts along dimension 0, may hold values from 2 to 8192, as said below
Outputs:
- attended: bfloat16 [256, 4096], P(('grp', 'seq')), parts along dimension 0
There are 2 independent parts, one for each index of `grp`. A program takes and returns all parts, laid end to end along the dimension named above; each array names one. Nothing has to cross between parts.
Inputs may be any that keep to these rules, and one draw needn't show every extreme that they name: Some question has offsets equal to 8192.
All inputs are finite; a program needn't handle non-finite values.
Results may differ from a plain program's by a relative error of at most 0.0029.
Values may be sent and summed in bfloat16 or wider, within the bound.
No kernel may reach another device: no remote copies, remote signals or barrier semaphores. Data moves between devices by JAX's collectives and lax.ppermute only.
A program may use at most 64 MiB of HBM per device.

v0:
```python
import math
import jax
import jax.numpy as jnp
from jax import lax
from jax.sharding import PartitionSpec as P

H = 32
KVH = 16
HD = 128
QSCALE = 144
QL = 128
NQ = 1
MASKED = -1e30


def row_tables(start, count, lengths, offsets):
    rows = start + jnp.arange(count, dtype=jnp.int32)
    question = rows // QL
    position = rows % QL
    owner_table = question[:, None] == jnp.arange(NQ, dtype=jnp.int32)[None, :]
    row_length = jnp.sum(jnp.where(owner_table, lengths[None, :], 0), axis=1)
    row_offset = jnp.sum(jnp.where(owner_table, offsets[None, :], 0), axis=1)
    return (question, position, position < row_length, row_offset)


def local(queries, question_keys, question_values, doc_keys, doc_values, lengths, offsets):
    rows_local = queries.shape[0]
    doc_local = doc_keys.shape[0]
    device_count = lax.axis_size("seq")
    device_index = lax.axis_index("seq")
    total_rows = rows_local * device_count
    per_group = H // KVH
    factor_q = QSCALE ** (-0.5)
    key_doc = doc_keys.reshape(doc_local, KVH, HD)
    value_doc = doc_values.reshape(doc_local, KVH, HD)
    key_self = question_keys.reshape(rows_local, KVH, HD)
    value_self = question_values.reshape(rows_local, KVH, HD)
    doc_places = device_index * doc_local + jnp.arange(doc_local, dtype=jnp.int32)
    self_rows = device_index * rows_local + jnp.arange(rows_local, dtype=jnp.int32)
    whole = lax.all_gather(queries, "seq", axis=0, tiled=True)
    block_rows = math.gcd(total_rows, 512)
    block_count = total_rows // block_rows

    def one_block(start):
        piece = whole.reshape(block_rows, KVH, per_group, HD)
        question, position, live_rows, row_offset = row_tables(start, block_rows, lengths, offsets)
        mask_doc = live_rows[:, None] & (doc_places[None, :] < row_offset[:, None])
        mask_self = (
            live_rows[:, None]
            & (self_rows[None, :] // QL == question[:, None])
            & (self_rows[None, :] % QL <= position[:, None])
        )
        mask_doc = mask_doc[:, None, None, :]
        mask_self = mask_self[:, None, None, :]
        scores_doc = (
            jnp.einsum("rgjd,kgd->rgjk", piece, key_doc, preferred_element_type=jnp.float32)
            * factor_q
        )
        scores_self = (
            jnp.einsum("rgjd,kgd->rgjk", piece, key_self, preferred_element_type=jnp.float32)
            * factor_q
        )
        scores_doc = jnp.where(mask_doc, scores_doc, MASKED)
        scores_self = jnp.where(mask_self, scores_self, MASKED)
        block_top = jnp.maximum(jnp.max(scores_doc, axis=-1), jnp.max(scores_self, axis=-1))
        weights_doc = jnp.where(mask_doc, jnp.exp(scores_doc - block_top[..., None]), 0.0).astype(
            jnp.bfloat16
        )
        weights_self = jnp.where(
            mask_self, jnp.exp(scores_self - block_top[..., None]), 0.0
        ).astype(jnp.bfloat16)
        block_den = jnp.sum(weights_doc.astype(jnp.float32), axis=-1) + jnp.sum(
            weights_self.astype(jnp.float32), axis=-1
        )
        block_num = jnp.einsum(
            "rgjk,kgd->rgjd", weights_doc, value_doc, preferred_element_type=jnp.float32
        )
        block_num = block_num + jnp.einsum(
            "rgjk,kgd->rgjd", weights_self, value_self, preferred_element_type=jnp.float32
        )
        return (
            block_num.reshape(block_rows, H * HD),
            block_top.reshape(block_rows, H),
            block_den.reshape(block_rows, H),
        )

    starts = jnp.arange(block_count, dtype=jnp.int32) * block_rows
    numer, row_top, denom = lax.map(one_block, starts)
    numer = numer.reshape(total_rows, H * HD)
    row_top = row_top.reshape(total_rows, H)
    denom = denom.reshape(total_rows, H)
    got_num, got_top, got_den = (
        lax.all_to_all(numer[None], "seq", split_axis=1, concat_axis=0, tiled=True),
        lax.all_to_all(row_top[None], "seq", split_axis=1, concat_axis=0, tiled=True),
        lax.all_to_all(denom[None], "seq", split_axis=1, concat_axis=0, tiled=True),
    )
    overall = jnp.max(got_top, axis=0)
    rescale = jnp.exp(got_top - overall[None])
    total_num = jnp.sum(
        got_num.reshape(device_count, rows_local, H, HD) * rescale[:, :, :, None], axis=0
    )
    total_den = jnp.sum(got_den * rescale, axis=0)
    question, position, live_rows, row_offset = row_tables(
        device_index * rows_local, rows_local, lengths, offsets
    )
    safe_den = jnp.where(live_rows[:, None], total_den, 1.0)
    result = (total_num / safe_den[:, :, None]).reshape(rows_local, H * HD)
    return jnp.where(live_rows[:, None], result, 0.0).astype(jnp.bfloat16)


def solution(mesh):
    placed = (
        P(("grp", "seq"), None),
        P(("grp", "seq"), None),
        P(("grp", "seq"), None),
        P(("grp", "seq"), None),
        P(("grp", "seq"), None),
        P("grp"),
        P("grp"),
    )
    return jax.shard_map(
        local, mesh=mesh, in_specs=placed, out_specs=P(("grp", "seq"), None), check_vma=False
    )
```

profile of v0, /device:TPU:13, one launch (start us, length us, event | category | flops | bytes accessed | tf_op | source)
XLA Modules:
  0.0 149.6 jit_solution(6486073147577093918)
XLA Ops:
  6.5 0.0 copy-start
  6.5 0.0 copy-start.2
  6.5 0.0 all-gather.2.cloned.1.call-start
  6.5 0.7 all-gather.2.cloned.1.call-update
  8.6 3.6 %copy.52 = bf16[64,8,16,128]{3,2,1,0:T(8,128)(2,1)} copy(bf16[64,8,16,128]{3,1,2,0:T(8,128)(2,1)} %bitcast.72) | data formatting | bytes 4194304
  12.1 0.0 copy-done.2
  12.1 0.0 copy-start.4
  12.1 2.5 %copy.50 = bf16[512,2048]{0,1:T(8,128)(2,1)} copy(bf16[512,2048]{1,0:T(8,128)(2,1)S(1)} %copy-done.2) | data formatting | bytes 4194304 | tf_op jit(solution)/shard_map/reshape | solution.py:35
  14.7 0.1 compare_and_fusion.1
  14.8 0.1 compare_and_fusion
  15.0 32.6 %all-gather.2.cloned.1.call-done = bf16[128,4096]{1,0:T(8,128)(2,1)} async-done(((bf16[8,4096]{1,0:T(8,128)(2,1)}), bf16[128,4096]{1,0:T(8,128)(2,1)}) %all-gather.2.cloned.1.call-update) | async-done | bytes 1048592 | tf_op jit(solution)/shard_map/all_gather | solution.py:40
  47.5 1.6 %copy.30 = bf16[128,4096]{0,1:T(8,128)(2,1)S(1)} copy(bf16[128,4096]{1,0:T(8,128)(2,1)} %all-gather.2.cloned.1.call-done) | data formatting | bytes 2097152 | tf_op jit(solution)/shard_map/all_gather | solution.py:40
  49.2 0.0 copy-done.4
  49.2 0.3 fusion.14
  49.4 3.2 %fusion = (f32[128,16,2]{0,2,1:T(2,128)S(1)}, f32[16,512,128,2]{2,1,3,0:T(8,128)S(1)}) fusion(pred[128,512]{0,1:T(8,128)(4,1)S(1)} %compare_and_fusion, bf16[128,16,2,128]{0,3,2,1:T(8,128)(2,1)S(1)} %bitcast.71, bf16[512,16,128,1]{2,1,0,3:T(8,128)(2,1)} %bitcast.74), kind=kOutput, calls=%fused_computation.3 | convolution fusion | flops 543158272 | bytes 11616256 | tf_op jit(solution)/shard_map/while/body/eval_jaxpr/rgjd,kgd->rgjk/dot_general | solution.py:56
  52.6 0.0 copy-start.1
  52.6 0.0 copy-start.3
  52.7 2.1 %convert_reduce_fusion = f32[128,16,2]{0,2,1:T(2,128)S(1)} fusion(f32[128,16,2]{0,2,1:T(2,128)S(1)} %max.18, f32[16,512,128,2]{2,1,3,0:T(8,128)S(1)} %get-tuple-element.32, pred[128,512]{0,1:T(8,128)(4,1)S(1)} %compare_and_fusion), kind=kLoop, calls=%fused_computation.1 | loop fusion | flops 14675968 | bytes 8486912 | tf_op jit(solution)/shard_map/while/body/eval_jaxpr/reduce_sum | solution.py:72
  54.7 1.4 copy-done.1
  56.2 0.1 convert_reduce_fusion.1
  56.3 0.1 copy.39
  56.4 0.6 broadcast.482
  56.9 0.8 reduce.1
  57.7 0.7 reshape.376
  58.4 5.4 %all-to-all-start.2 = ((f32[16,1,256]{2,1,0:T(1,128)}), f32[16,1,256]{2,1,0:T(1,128)S(1)}, u32[]{:S(2)}, u32[]{:S(2)}) async-start(f32[16,1,256]{2,1,0:T(1,128)} %reshape.376), calls=%async_computation.2 | async-start | bytes 32768 | tf_op jit(solution)/shard_map/all_to_all | solution.py:95
  63.8 0.0 copy-done
  63.8 1.8 %fusion.8 = f32[16,128,2,128]{1,3,2,0:T(8,128)} fusion(bf16[8,2048]{1,0:T(8,128)(2,1)S(1)} %copy-done, f32[128,16,2,8]{0,3,2,1:T(8,128)S(1)} %get-tuple-element.34, f32[128,16,2]{0,2,1:T(2,128)S(1)} %max.18, pred[128,8]{0,1:T(8,128)(4,1)S(1)} %compare_and_fusion.1), kind=kOutput, calls=%fused_computation.20 | convolution fusion | flops 8486912 | bytes 2278400 | tf_op jit(solution)/shard_map/while/body/eval_jaxpr/rgjk,kgd->rgjd/dot_general | solution.py:78
  65.6 0.1 copy.37
  65.7 0.8 reduce.3
  66.5 0.7 reshape.374
  67.2 0.8 all-to-all-done.2
  67.9 5.8 %all-to-all-start.1 = ((f32[16,1,256]{2,1,0:T(1,128)}), f32[16,1,256]{2,1,0:T(1,128)S(1)}, u32[]{:S(2)}, u32[]{:S(2)}) async-start(f32[16,1,256]{2,1,0:T(1,128)} %reshape.374), calls=%async_computation.1 | async-start | bytes 32768 | tf_op jit(solution)/shard_map/all_to_all | solution.py:94
  73.7 0.0 copy-done.3
  73.7 7.3 %convolution_add_fusion = f32[16,128,2,128]{1,3,2,0:T(8,128)} fusion(f32[16,128,2,128]{1,3,2,0:T(8,128)} %fusion.8, bf16[512,16,128,1]{0,2,3,1:T(8,128)(2,1)S(1)} %bitcast.73, f32[16,512,128,2]{2,1,3,0:T(8,128)} %copy-done.1, f32[128,16,2]{0,2,1:T(2,128)S(1)} %max.18, pred[128,512]{0,1:T(8,128)(4,1)S(1)} %compare_and_fusion), kind=kOutput, calls=%fused_computation.8 | convolution fusion | flops 547880960 | bytes 14761984 | tf_op jit(solution)/shard_map/while/body/eval_jaxpr/rgjk,kgd->rgjd/dot_general | solution.py:75
  81.0 5.7 %copy.36 = f32[1,128,4096]{2,0,1:T(1,128)} copy(f32[1,128,4096]{1,2,0:T(8,128)} %bitcast.75) | data formatting | bytes 4194304 | tf_op jit(solution)/shard_map/while/body/jit(dynamic_update_index_in_dim)/broadcast_in_dim | solution.py:88
  86.7 0.0 all-to-all-done.1
  86.7 6.1 %all-to-all-start = ((f32[1,128,4096]{2,0,1:T(1,128)}), f32[1,128,4096]{2,0,1:T(1,128)S(1)}, u32[]{:S(2)}, u32[]{:S(2)}) async-start(f32[1,128,4096]{2,0,1:T(1,128)} %copy.36), calls=%async_computation | async-start | bytes 4194304 | tf_op jit(solution)/shard_map/all_to_all | solution.py:93
  92.8 0.7 reduce.2
  93.4 0.1 reshape.377
  93.6 0.7 reduce.4
  94.2 0.1 reshape.375
  94.4 0.1 copy.38
  94.6 0.1 broadcast_select_fusion
  94.6 0.1 copy.40
  94.7 45.4 %all-to-all-done = f32[1,128,4096]{2,0,1:T(1,128)S(1)} async-done(((f32[1,128,4096]{2,0,1:T(1,128)}), f32[1,128,4096]{2,0,1:T(1,128)S(1)}, u32[]{:S(2)}, u32[]{:S(2)}) %all-to-all-start) | async-done | bytes 2097184 | tf_op jit(solution)/shard_map/all_to_all | solution.py:93
  140.2 1.8 %fusion.1 = f32[8,4096]{1,0:T(8,128)S(1)} fusion(f32[1,128,4096]{2,0,1:T(1,128)S(1)} %all-to-all-done, f32[16,8,32]{1,2,0:T(8,128)S(1)} %copy.38), kind=kLoop, calls=%fused_computation.5 | loop fusion | flops 1015808 | bytes 2244608 | tf_op jit(solution)/shard_map/reduce_sum | solution.py:99
  142.0 0.7 fusion.7
  (10 shorter events, 0.1 us)
Async XLA Ops:
  6.5 57.3 %copy-start = (bf16[8,2048]{1,0:T(8,128)(2,1)S(1)}, bf16[8,2048]{1,0:T(8,128)(2,1)}, u32[]{:S(2)}) copy-start(bf16[8,2048]{1,0:T(8,128)(2,1)} %param.9) | copy-start | bytes 98308
  6.5 5.6 %copy-start.2 = (bf16[512,2048]{1,0:T(8,128)(2,1)S(1)}, bf16[512,2048]{1,0:T(8,128)(2,1)}, u32[]{:S(2)}) copy-start(bf16[512,2048]{1,0:T(8,128)(2,1)} %param.11) | copy-start | bytes 6291460
  6.5 41.0 %all-gather.2.cloned.1.call-start = ((), (), s32[]{:S(2)}) async-start(), calls=%async_computation.3 | async-start | bytes 1114112 | tf_op jit(solution)/shard_map/all_gather | solution.py:40
  12.1 37.0 %copy-start.4 = (bf16[8,2048]{1,0:T(8,128)(2,1)S(1)}, bf16[8,2048]{1,0:T(8,128)(2,1)}, u32[]{:S(2)}) copy-start(bf16[8,2048]{1,0:T(8,128)(2,1)} %param.8) | copy-start | bytes 98308
  52.6 3.6 %copy-start.1 = (f32[16,512,128,2]{2,1,3,0:T(8,128)}, f32[16,512,128,2]{2,1,3,0:T(8,128)S(1)}, u32[]{:S(2)}) copy-start(f32[16,512,128,2]{2,1,3,0:T(8,128)S(1)} %get-tuple-element.32) | copy-start | bytes 25165828
  52.6 21.1 %copy-start.3 = (bf16[512,2048]{0,1:T(8,128)(2,1)S(1)}, bf16[512,2048]{0,1:T(8,128)(2,1)}, u32[]{:S(2)}) copy-start(bf16[512,2048]{0,1:T(8,128)(2,1)} %copy.50) | copy-start | bytes 6291460
  58.4 9.5 %all-to-all-start.2 = ((f32[16,1,256]{2,1,0:T(1,128)}), f32[16,1,256]{2,1,0:T(1,128)S(1)}, u32[]{:S(2)}, u32[]{:S(2)}) async-start(f32[16,1,256]{2,1,0:T(1,128)} %reshape.376), calls=%async_computation.2 | async-start | bytes 32768 | tf_op jit(solution)/shard_map/all_to_all | solution.py:95
  67.9 18.7 %all-to-all-start.1 = ((f32[16,1,256]{2,1,0:T(1,128)}), f32[16,1,256]{2,1,0:T(1,128)S(1)}, u32[]{:S(2)}, u32[]{:S(2)}) async-start(f32[16,1,256]{2,1,0:T(1,128)} %reshape.374), calls=%async_computation.1 | async-start | bytes 32768 | tf_op jit(solution)/shard_map/all_to_all | solution.py:94
  86.7 53.5 %all-to-all-start = ((f32[1,128,4096]{2,0,1:T(1,128)}), f32[1,128,4096]{2,0,1:T(1,128)S(1)}, u32[]{:S(2)}, u32[]{:S(2)}) async-start(f32[1,128,4096]{2,0,1:T(1,128)} %copy.36), calls=%async_computation | async-start | bytes 4194304 | tf_op jit(solution)/shard_map/all_to_all | solution.py:93
Sparse Core Ops, SparseCore 0:
  9.5 38.0 all-gather.1
where the time goes:
time: 150 us
  waiting for transfers between devices  79.5 us (53%)
  local copies, waits for them, and re-layouts  17.5 us (12%)
  starting transfers between devices  17.2 us (11%)
  between operations  14.9 us (10%)
  matrix products  12.5 us (8%)
  other arithmetic  7.99 us (5%)
    all_to_all x1, waiting for transfers between devices, local(): lax.all_to_all(numer[None], 'seq', split_axis=1, concat_axis=0, tiled=True)  45.4 us
    all_gather x1, waiting for transfers between devices, local(): whole = lax.all_gather(queries, 'seq', axis=0, tiled=True)  32.6 us
    dot_general x1, matrix products, one_block(): jnp.einsum('rgjk,kgd->rgjd', weights_doc, value_doc, preferred_element_ty...  7.29 us
    unnamed x16, local copies, waits for them, and re-layouts  7.29 us
    all_to_all x1, starting transfers between devices, local(): lax.all_to_all(numer[None], 'seq', split_axis=1, concat_axis=0, tiled=True)  6.06 us
    all_to_all x1, starting transfers between devices, local(): lax.all_to_all(row_top[None], 'seq', split_axis=1, concat_axis=0, tiled=T...  5.76 us
    broadcast_in_dim x1, local copies, waits for them, and re-layouts, local(): numer, row_top, denom = lax.map(one_block, starts)  5.68 us
    all_to_all x1, starting transfers between devices, local(): lax.all_to_all(denom[None], 'seq', split_axis=1, concat_axis=0, tiled=True)  5.37 us
  transfers between devices with their start and end apart: 4, of which 3 were waited for; matrix products, arithmetic and copies ran while one was open for 16% of the time, Pallas kernels for 0%

commit v1 on v0

--- a/solution.py
+++ b/solution.py
@@ -90,7 +90,12 @@
     row_top = row_top.reshape(total_rows, H)
     denom = denom.reshape(total_rows, H)
     got_num, got_top, got_den = (
-        lax.all_to_all(numer[None], "seq", split_axis=1, concat_axis=0, tiled=True),
+        jnp.concatenate(
+            lax.all_to_all(
+                jnp.stack(jnp.split(numer[None], lax.axis_size("seq"), axis=1)), "seq", 0, 0
+            ),
+            axis=0,
+        ),
         lax.all_to_all(row_top[None], "seq", split_axis=1, concat_axis=0, tiled=True),
         lax.all_to_all(denom[None], "seq", split_axis=1, concat_axis=0, tiled=True),
     )

time: 150 us -> 206 us (1.37)
  local copies, waits for them, and re-layouts: 17.5 us -> 76.3 us
  matrix products: 12.5 us -> 7.81 us
  waiting for transfers between devices: 79.5 us -> 82 us
    unnamed x16 -> x49, local copies, waits for them, and re-layouts: 7.29 us -> 57.7 us
    split x0 -> x1, local copies, waits for them, and re-layouts: none -> 13.3 us  [local(): jnp.split(numer[None], lax.axis_size('seq'), axis=1)]
    broadcast_in_dim x1 -> x0, local copies, waits for them, and re-layouts: 5.68 us -> none  [local(): numer, row_top, denom = lax.map(one_block, starts)]
    all_to_all x1, waiting for transfers between devices: 0.01 us -> 3.48 us  [local(): lax.all_to_all(row_top[None], 'seq', split_axis=1, concat_axis=0, tiled=T...]
  transfers between devices with their start and end apart: 4 -> 4, of which waited for: 3 -> 3; matrix products, arithmetic and copies ran while one was open for 16% -> 39% of each run, Pallas kernels for 0% -> 0%
where the time goes in v1:
time: 206 us; the launch traced here: 205 us
  waiting for transfers between devices  82 us (40%)
  local copies, waits for them, and re-layouts  76.3 us (37%)
  starting transfers between devices  17.4 us (8%)
  between operations  14.9 us (7%)
  matrix products  7.81 us (4%)
  other arithmetic  6.94 us (3%)
    unnamed x49, local copies, waits for them, and re-layouts  57.7 us
    all_to_all x1, waiting for transfers between devices, local(): lax.all_to_all(jnp.stack(jnp.split(numer[None], lax.axis_size('seq'), axi...  45.4 us
    all_gather x1, waiting for transfers between devices, local(): whole = lax.all_gather(queries, 'seq', axis=0, tiled=True)  32.4 us
    split x1, local copies, waits for them, and re-layouts, local(): jnp.split(numer[None], lax.axis_size('seq'), axis=1)  13.3 us
    all_to_all x1, starting transfers between devices, local(): lax.all_to_all(row_top[None], 'seq', split_axis=1, concat_axis=0, tiled=T...  6.03 us
    all_to_all x1, starting transfers between devices, local(): lax.all_to_all(jnp.stack(jnp.split(numer[None], lax.axis_size('seq'), axi...  6 us
    dot_general x1, matrix products, one_block(): jnp.einsum('rgjk,kgd->rgjd', weights_doc, value_doc, preferred_element_ty...  5.48 us
    all_to_all x1, starting transfers between devices, local(): lax.all_to_all(denom[None], 'seq', split_axis=1, concat_axis=0, tiled=True)  5.37 us
  transfers between devices with their start and end apart: 4, of which 3 were waited for; matrix products, arithmetic and copies ran while one was open for 39% of the time, Pallas kernels for 0%

profile of v1, /device:TPU:13, one launch (start us, length us, event | category | flops | bytes accessed | tf_op | source)
XLA Modules:
  0.0 205.3 jit_solution(3214430472673109701)
XLA Ops:
  6.5 0.7 all-gather.2.cloned.1.call-update
  8.6 3.7 %copy.112 = bf16[64,8,16,128]{3,2,1,0:T(8,128)(2,1)} copy(bf16[64,8,16,128]{3,1,2,0:T(8,128)(2,1)} %bitcast.103) | data formatting | bytes 4194304
  12.3 2.5 %copy.94 = bf16[512,2048]{0,1:T(8,128)(2,1)} copy(bf16[512,2048]{1,0:T(8,128)(2,1)S(1)} %copy-done.2) | data formatting | bytes 4194304 | tf_op jit(solution)/shard_map/reshape | solution.py:35
  15.1 32.4 %all-gather.2.cloned.1.call-done = bf16[128,4096]{1,0:T(8,128)(2,1)} async-done(((bf16[8,4096]{1,0:T(8,128)(2,1)}), bf16[128,4096]{1,0:T(8,128)(2,1)}) %all-gather.2.cloned.1.call-update) | async-done | bytes 1048592 | tf_op jit(solution)/shard_map/all_gather | solution.py:40
  47.5 1.6 copy.57
  49.5 1.6 fusion
  51.1 2.1 %convert_reduce_fusion = f32[128,16,2]{0,2,1:T(2,128)S(1)} fusion(f32[128,16,2]{0,2,1:T(2,128)S(1)} %max.18, f32[16,512,128,2]{2,1,3,0:T(8,128)S(1)} %get-tuple-element.63, pred[128,512]{0,1:T(8,128)(4,1)S(1)} %compare_and_fusion), kind=kLoop, calls=%fused_computation.1 | loop fusion | flops 14675968 | bytes 8486912 | tf_op jit(solution)/shard_map/while/body/eval_jaxpr/reduce_sum | solution.py:72
  53.1 1.1 copy-done.1
  55.0 0.8 reduce.1
  55.8 0.7 reshape.354
  56.5 5.4 %all-to-all-start.2 = ((f32[16,1,256]{2,1,0:T(1,128)}), f32[16,1,256]{2,1,0:T(1,128)S(1)}, u32[]{:S(2)}, u32[]{:S(2)}) async-start(f32[16,1,256]{2,1,0:T(1,128)} %reshape.354), calls=%async_computation.2 | async-start | bytes 32768 | tf_op jit(solution)/shard_map/all_to_all | solution.py:100
  62.4 5.5 %convolution_add_fusion = f32[16,128,2,128]{1,3,2,0:T(8,128)S(1)} fusion(f32[16,128,2,128]{1,3,2,0:T(8,128)S(1)} %fusion.8, bf16[512,16,128,1]{0,2,3,1:T(8,128)(2,1)S(1)} %bitcast.104, f32[16,512,128,2]{2,1,3,0:T(8,128)} %copy-done.1, f32[128,16,2]{0,2,1:T(2,128)S(1)} %max.18, pred[128,512]{0,1:T(8,128)(4,1)S(1)} %compare_and_fusion), kind=kOutput, calls=%fused_computation.8 | convolution fusion | flops 547880960 | bytes 14761984 | tf_op jit(solution)/shard_map/while/body/eval_jaxpr/rgjk,kgd->rgjd/dot_general | solution.py:75
  67.9 13.3 %fusion.14 = (f32[1,8,4096]{1,2,0:T(8,128)S(1)}, f32[1,8,4096]{1,2,0:T(8,128)}, f32[1,8,4096]{1,2,0:T(8,128)}, f32[1,8,4096]{1,2,0:T(8,128)}, f32[1,8,4096]{1,2,...) fusion(f32[1,128,4096]{1,2,0:T(8,128)S(1)} %bitcast.100), kind=kLoop, calls=%fused_computation.59 | loop fusion | bytes 4194304 | tf_op jit(solution)/shard_map/split | solution.py:95
  81.2 2.2 %copy.110 = f32[1,8,4096]{2,1,0:T(8,128)S(1)} copy(f32[1,8,4096]{1,2,0:T(8,128)} %get-tuple-element.32) | data formatting | bytes 262144
  83.3 2.2 %copy.109 = f32[1,8,4096]{2,1,0:T(8,128)S(1)} copy(f32[1,8,4096]{1,2,0:T(8,128)} %get-tuple-element.33) | data formatting | bytes 262144
  85.5 2.2 %copy.108 = f32[1,8,4096]{2,1,0:T(8,128)S(1)} copy(f32[1,8,4096]{1,2,0:T(8,128)} %get-tuple-element.34) | data formatting | bytes 262144
  87.7 2.2 %copy.107 = f32[1,8,4096]{2,1,0:T(8,128)S(1)} copy(f32[1,8,4096]{1,2,0:T(8,128)} %get-tuple-element.35) | data formatting | bytes 262144
  89.8 2.2 %copy.106 = f32[1,8,4096]{2,1,0:T(8,128)S(1)} copy(f32[1,8,4096]{1,2,0:T(8,128)} %get-tuple-element.36) | data formatting | bytes 262144
  92.0 2.2 %copy.105 = f32[1,8,4096]{2,1,0:T(8,128)S(1)} copy(f32[1,8,4096]{1,2,0:T(8,128)} %get-tuple-element.37) | data formatting | bytes 262144
  94.2 2.2 %copy.104 = f32[1,8,4096]{2,1,0:T(8,128)S(1)} copy(f32[1,8,4096]{1,2,0:T(8,128)} %get-tuple-element.38) | data formatting | bytes 262144
  96.3 2.2 %copy.103 = f32[1,8,4096]{2,1,0:T(8,128)S(1)} copy(f32[1,8,4096]{1,2,0:T(8,128)} %get-tuple-element.52) | data formatting | bytes 262144
  98.5 2.2 %copy.102 = f32[1,8,4096]{2,1,0:T(8,128)S(1)} copy(f32[1,8,4096]{1,2,0:T(8,128)} %get-tuple-element.54) | data formatting | bytes 262144
  100.7 2.2 %copy.101 = f32[1,8,4096]{2,1,0:T(8,128)S(1)} copy(f32[1,8,4096]{1,2,0:T(8,128)} %get-tuple-element.56) | data formatting | bytes 262144
  102.8 2.8 %copy.100 = f32[1,8,4096]{2,1,0:T(8,128)} copy(f32[1,8,4096]{1,2,0:T(8,128)} %get-tuple-element.57) | data formatting | bytes 262144
  105.7 2.8 %copy.99 = f32[1,8,4096]{2,1,0:T(8,128)} copy(f32[1,8,4096]{1,2,0:T(8,128)} %get-tuple-element.58) | data formatting | bytes 262144
  108.5 2.8 %copy.98 = f32[1,8,4096]{2,1,0:T(8,128)} copy(f32[1,8,4096]{1,2,0:T(8,128)} %get-tuple-element.59) | data formatting | bytes 262144
  111.3 2.8 %copy.97 = f32[1,8,4096]{2,1,0:T(8,128)} copy(f32[1,8,4096]{1,2,0:T(8,128)} %get-tuple-element.60) | data formatting | bytes 262144
  114.1 2.8 %copy.96 = f32[1,8,4096]{2,1,0:T(8,128)} copy(f32[1,8,4096]{1,2,0:T(8,128)} %get-tuple-element.61) | data formatting | bytes 262144
  116.9 1.5 bitcast_dynamic-update-slice_fusion.15
  118.4 1.6 bitcast_dynamic-update-slice_fusion.14
  120.0 1.6 bitcast_dynamic-update-slice_fusion.13
  121.6 1.6 bitcast_dynamic-update-slice_fusion.12
  123.1 1.6 bitcast_dynamic-update-slice_fusion.11
  126.0 0.7 bitcast_dynamic-update-slice_fusion.8
  127.3 0.7 bitcast_dynamic-update-slice_fusion.6
  128.6 0.7 bitcast_dynamic-update-slice_fusion.4
  130.0 0.7 bitcast_dynamic-update-slice_fusion.2
  131.4 0.8 reduce.3
  132.2 0.7 reshape.352
  133.4 6.0 %all-to-all-start.1 = ((f32[16,1,256]{2,1,0:T(1,128)}), f32[16,1,256]{2,1,0:T(1,128)S(1)}, u32[]{:S(2)}, u32[]{:S(2)}) async-start(f32[16,1,256]{2,1,0:T(1,128)} %reshape.352), calls=%async_computation.1 | async-start | bytes 32768 | tf_op jit(solution)/shard_map/all_to_all | solution.py:99
  139.5 0.7 bitcast_dynamic-update-slice_fusion
  140.1 3.5 %all-to-all-done.1 = f32[16,1,256]{2,1,0:T(1,128)S(1)} async-done(((f32[16,1,256]{2,1,0:T(1,128)}), f32[16,1,256]{2,1,0:T(1,128)S(1)}, u32[]{:S(2)}, u32[]{:S(2)}) %all-to-all-start.1) | async-done | bytes 16416 | tf_op jit(solution)/shard_map/all_to_all | solution.py:99
  143.6 6.0 %all-to-all-start = ((f32[16,1,8,4096]{3,2,1,0:T(8,128)}), f32[16,1,8,4096]{3,2,1,0:T(8,128)S(1)}, u32[]{:S(2)}, u32[]{:S(2)}) async-start(f32[16,1,8,4096]{3,2,1,0:T(8,128)} %bitcast_dynamic-update-slice_fusion), calls=%async_computation | async-start | bytes 4194304 | tf_op jit(solution)/shard_map/all_to_all | solution.py:94
  149.6 0.7 reduce.2
  150.5 0.7 reduce.4
  151.6 45.4 %all-to-all-done = f32[16,1,8,4096]{3,2,1,0:T(8,128)S(1)} async-done(((f32[16,1,8,4096]{3,2,1,0:T(8,128)}), f32[16,1,8,4096]{3,2,1,0:T(8,128)S(1)}, u32[]{:S(2)}, u32[]{:S(2)}) %all-to-all-start) | async-done | bytes 2097184 | tf_op jit(solution)/shard_map/all_to_all | solution.py:94
  197.0 0.7 fusion.1
  197.8 0.7 fusion.7
  (43 shorter events, 7.0 us)
Async XLA Ops:
  6.5 55.4 %copy-start = (bf16[8,2048]{1,0:T(8,128)(2,1)S(1)}, bf16[8,2048]{1,0:T(8,128)(2,1)}, u32[]{:S(2)}) copy-start(bf16[8,2048]{1,0:T(8,128)(2,1)} %param.9) | copy-start | bytes 98308
  6.5 41.0 %all-gather.2.cloned.1.call-start = ((), (), s32[]{:S(2)}) async-start(), calls=%async_computation.3 | async-start | bytes 1114112 | tf_op jit(solution)/shard_map/all_gather | solution.py:40
  8.6 3.7 %copy-start.2 = (bf16[512,2048]{1,0:T(8,128)(2,1)S(1)}, bf16[512,2048]{1,0:T(8,128)(2,1)}, u32[]{:S(2)}) copy-start(bf16[512,2048]{1,0:T(8,128)(2,1)} %param.11) | copy-start | bytes 6291460
  14.8 34.3 %copy-start.5 = (bf16[8,2048]{1,0:T(8,128)(2,1)S(1)}, bf16[8,2048]{1,0:T(8,128)(2,1)}, u32[]{:S(2)}) copy-start(bf16[8,2048]{1,0:T(8,128)(2,1)} %param.8) | copy-start | bytes 98308
  14.8 34.6 %copy-start.4 = (bf16[64,8,16,128]{3,2,1,0:T(8,128)(2,1)S(1)}, bf16[64,8,16,128]{3,2,1,0:T(8,128)(2,1)}, u32[]{:S(2)}) copy-start(bf16[64,8,16,128]{3,2,1,0:T(8,128)(2,1)} %copy.112) | copy-start | bytes 6291460
  51.0 3.2 %copy-start.1 = (f32[16,512,128,2]{2,1,3,0:T(8,128)}, f32[16,512,128,2]{2,1,3,0:T(8,128)S(1)}, u32[]{:S(2)}) copy-start(f32[16,512,128,2]{2,1,3,0:T(8,128)S(1)} %get-tuple-element.63) | copy-start | bytes 25165828
  54.3 8.1 %copy-start.3 = (bf16[512,2048]{0,1:T(8,128)(2,1)S(1)}, bf16[512,2048]{0,1:T(8,128)(2,1)}, u32[]{:S(2)}) copy-start(bf16[512,2048]{0,1:T(8,128)(2,1)} %copy.94) | copy-start | bytes 6291460
  56.5 76.9 %all-to-all-start.2 = ((f32[16,1,256]{2,1,0:T(1,128)}), f32[16,1,256]{2,1,0:T(1,128)S(1)}, u32[]{:S(2)}, u32[]{:S(2)}) async-start(f32[16,1,256]{2,1,0:T(1,128)} %reshape.354), calls=%async_computation.2 | async-start | bytes 32768 | tf_op jit(solution)/shard_map/all_to_all | solution.py:100
  133.4 10.2 %all-to-all-start.1 = ((f32[16,1,256]{2,1,0:T(1,128)}), f32[16,1,256]{2,1,0:T(1,128)S(1)}, u32[]{:S(2)}, u32[]{:S(2)}) async-start(f32[16,1,256]{2,1,0:T(1,128)} %reshape.352), calls=%async_computation.1 | async-start | bytes 32768 | tf_op jit(solution)/shard_map/all_to_all | solution.py:99
  143.6 53.4 %all-to-all-start = ((f32[16,1,8,4096]{3,2,1,0:T(8,128)}), f32[16,1,8,4096]{3,2,1,0:T(8,128)S(1)}, u32[]{:S(2)}, u32[]{:S(2)}) async-start(f32[16,1,8,4096]{3,2,1,0:T(8,128)} %bitcast_dynamic-update-slice_fusion), calls=%async_computation | async-start | bytes 4194304 | tf_op jit(solution)/shard_map/all_to_all | solution.py:94
Sparse Core Ops, SparseCore 0:
  9.5 38.0 all-gather.1
